TPU v7x, 16 devices: a 4x2x1 block of a 4x4x8 slice. The times are simulated.
16 devices in a mesh: dp: 4 (over y, z, core), tp: 4 (over x).
Axes of the slice: x: 4, y: 2, z: 1, core: 2. Of those that a mesh axis runs over, the one named last changes fastest.
The devices are a block of a 4x4x8 slice.
Arguments:
- x: bfloat16 [3584, 5120], P(('dp', 'tp')), parts along dimension 0
- w_gate: bfloat16 [5120, 17408], P(None, 'tp')
- w_up: bfloat16 [5120, 17408], P(None, 'tp')
- w_down: bfloat16 [17408, 5120], P('tp')
Outputs:
- output: bfloat16 [3584, 5120], P(('dp', 'tp')), parts along dimension 0
There are 4 independent parts. A program takes and returns all parts, laid end to end along the dimension named above; an argument that names none is the same for every part.
All inputs are finite; a program needn't handle non-finite values.
Results may differ from a plain program's by a relative error of at most 0.016.
Values are sent between devices in bfloat16 or wider.
A program may use at most 768 MiB of HBM per device.

v0:
```python
import jax
import jax.numpy as jnp
from jax import lax
from jax.sharding import PartitionSpec as P


def solution(mesh):
    def step(x, w_gate, w_up, w_down):
        rows = lax.all_gather(x, "tp", axis=0, tiled=True)
        gate = jnp.dot(rows, w_gate, preferred_element_type=jnp.float32)
        up = jnp.dot(rows, w_up, preferred_element_type=jnp.float32)
        hidden = (jax.nn.silu(gate) * up).astype(jnp.bfloat16)
        term = jnp.dot(hidden, w_down, preferred_element_type=jnp.float32).astype(jnp.bfloat16)
        return lax.psum_scatter(term, "tp", scatter_dimension=0, tiled=True)

    return jax.shard_map(
        step,
        mesh=mesh,
        in_specs=(P(("dp", "tp"), None), P(None, "tp"), P(None, "tp"), P("tp", None)),
        out_specs=P(("dp", "tp"), None),
        check_vma=False,
    )
```

profile of v0, /device:TPU:112, one launch (start us, length us, event | category | flops | bytes accessed | tf_op | source)
XLA Modules:
  0.0 339.7 jit_solution(17914667586526225704)
XLA Ops:
  6.5 0.0 all-gather.2.cloned.1.call-start
  6.6 0.7 all-gather.2.cloned.1.call-update
  7.3 0.1 reduce-scatter.2.cloned.1.call-start
  7.4 90.4 %all-gather.2.cloned.1.call-done = bf16[896,5120]{1,0:T(8,128)(2,1)} async-done(((bf16[224,5120]{1,0:T(8,128)(2,1)}), bf16[896,5120]{1,0:T(8,128)(2,1)}) %all-gather.2.cloned.1.call-update) | async-done | bytes 9175056 | tf_op jit(solution)/shard_map/all_gather | solution.py:9
  97.7 0.0 copy-start
  97.7 53.0 %fusion = f32[896,4352]{1,0:T(8,128)} fusion(bf16[896,5120]{1,0:T(8,128)(2,1)} %all-gather.2.cloned.1.call-done, bf16[5120,4352]{1,0:T(8,128)(2,1)} %param.5), kind=kOutput, calls=%fused_computation.2 | convolution fusion | flops 39929774080 | bytes 69337088 | tf_op jit(solution)/shard_map/dot_general | solution.py:10
  150.7 0.0 copy-done
  150.7 50.0 %multiply_convert_fusion = bf16[896,4352]{1,0:T(8,128)(2,1)} fusion(f32[896,4352]{1,0:T(8,128)} %fusion, bf16[896,5120]{1,0:T(8,128)(2,1)S(1)} %copy-done, bf16[5120,4352]{1,0:T(8,128)(2,1)} %param.6), kind=kOutput, calls=%fused_computation | convolution fusion | flops 39953170432 | bytes 77135872 | tf_op jit(solution)/shard_map/dot_general | solution.py:11
  200.7 48.2 %convolution_convert_fusion = bf16[896,5120]{1,0:T(8,128)(2,1)} fusion(bf16[896,4352]{1,0:T(8,128)(2,1)} %multiply_convert_fusion, bf16[4352,5120]{1,0:T(8,128)(2,1)} %param.7), kind=kOutput, calls=%fused_computation.1 | convolution fusion | flops 39934361600 | bytes 61538304 | tf_op jit(solution)/shard_map/dot_general | solution.py:13
  248.9 0.1 reduce-scatter.2.cloned.1.call-update
  248.9 83.9 %reduce-scatter.2.cloned.1.call-done = bf16[224,5120]{1,0:T(8,128)(2,1)} async-done(((bf16[896,5120]{1,0:T(8,128)(2,1)}), bf16[224,5120]{1,0:T(8,128)(2,1)}) %reduce-scatter.2.cloned.1.call-update) | async-done | bytes 2293776 | tf_op jit(solution)/shard_map/reduce_scatter | solution.py:14
Async XLA Ops:
  6.5 91.2 %all-gather.2.cloned.1.call-start = ((), (), s32[]{:S(2)}) async-start(), calls=%async_computation.1 | async-start | bytes 11468800 | tf_op jit(solution)/shard_map/all_gather | solution.py:9
  7.3 325.5 %reduce-scatter.2.cloned.1.call-start = ((), (), s32[]{:S(2)}) async-start(), calls=%async_computation.2 | async-start | bytes 11468800 | tf_op jit(solution)/shard_map/reduce_scatter | solution.py:14
  97.7 53.0 %copy-start = (bf16[896,5120]{1,0:T(8,128)(2,1)S(1)}, bf16[896,5120]{1,0:T(8,128)(2,1)}, u32[]{:S(2)}) copy-start(bf16[896,5120]{1,0:T(8,128)(2,1)} %all-gather.2.cloned.1.call-done) | copy-start | bytes 27525124
Sparse Core Ops, SparseCore 0:
  8.9 88.7 all-gather.1
  249.1 83.7 reduce-scatter.1
where the time goes:
time: 340 us
  waiting for transfers between devices  175 us (51%)
  matrix products  151 us (44%)
  between operations  13.4 us (4%)
    all_gather x1, waiting for transfers between devices, step(): rows = lax.all_gather(x, 'tp', axis=0, tiled=True)  90.4 us
    reduce_scatter x1, waiting for transfers between devices, step(): return lax.psum_scatter(term, 'tp', scatter_dimension=0, tiled=True)  83.9 us
    dot_general x1, matrix products, step(): gate = jnp.dot(rows, w_gate, preferred_element_type=jnp.float32)  53 us
    dot_general x1, matrix products, step(): up = jnp.dot(rows, w_up, preferred_element_type=jnp.float32)  50 us
    dot_general x1, matrix products, step(): jnp.dot(hidden, w_down, preferred_element_type=jnp.float32)  48.2 us
  transfers between devices with their start and end apart: 2, of which 2 were waited for; matrix products, arithmetic and copies ran while one was open for 0% of the time, Pallas kernels for 0%

commit v1 on v0

v1 whole, which is shorter than its diff:
```python
import functools

import jax
import jax.numpy as jnp
from jax import lax
from jax.experimental import pallas as pl
from jax.experimental.pallas import tpu as pltpu
from jax.sharding import PartitionSpec as P

BF = jnp.bfloat16
F32 = jnp.float32
MESH = pl.DeviceIdType.MESH
SLOTS = 4
TF = 256
TN = 512
CHUNK = (80, 80, 64)
PIECES = ((0, 0, 48), (0, 48, 32), (1, 0, 48), (1, 48, 32), (2, 0, 32), (2, 32, 32))
LEFT, RIGHT = 0, 1
DIAG, DIRECT, SUM = 0, 1, 2


def _kernel(
    x, wg, wu, wd, y,
    xown, xc, h, ring, ds, dg, st, rc, lsum, yown,
    xsem, wsem, ag_s, ag_r, fw_s, fw_r, rs_s, rs_r,
):
    rows, d = x.shape
    ff = wg.shape[1]
    half = d // 2
    n_gu = ff // TF
    pairs = half // TN
    n_dn = 2 * pairs
    start_row = [sum(CHUNK[:c]) for c in range(len(CHUNK))]
    top = 3 * max(CHUNK)

    me = lax.axis_index("tp")
    n = lax.axis_size("tp")
    peer = (lax.rem(me + n - 1, n), lax.rem(me + 1, n))

    def remote(src, dst, ssem, rsem, way):
        return pltpu.make_async_remote_copy(
            src_ref=src, dst_ref=dst, send_sem=ssem, recv_sem=rsem,
            device_id={"tp": peer[way]}, device_id_type=MESH,
        )

    def gu_copies(i, slot):
        cols = pl.ds(pl.multiple_of(i * TF, TF), TF)
        return (
            pltpu.make_async_copy(wg.at[:, cols], ring.at[slot, :, pl.ds(0, TF)], wsem.at[slot, 0]),
            pltpu.make_async_copy(wu.at[:, cols], ring.at[slot, :, pl.ds(TF, TF)], wsem.at[slot, 1]),
        )

    def dn_cols(t):
        return lax.rem(t, 2) * half + (t // 2) * TN

    def dn_copies(t, slot):
        cols = pl.ds(pl.multiple_of(dn_cols(t), TN), TN)
        return (pltpu.make_async_copy(wd.at[:, cols], ring.at[slot, pl.ds(0, ff), :], wsem.at[slot, 0]),)

    def fetch(kind, i, slot):
        for c in (gu_copies if kind == "gu" else dn_copies)(i, slot):
            c.start()

    def next_fetch(kind, count, nxt, i, slot):
        ahead = i + SLOTS - 1
        to = lax.rem(slot + SLOTS - 1, SLOTS)

        @pl.when(ahead < count)
        def _():
            fetch(kind, ahead, to)

        if nxt is not None:
            @pl.when(ahead >= count)
            def _():
                fetch(nxt, ahead - count, to)

    def own_piece(p, way):
        c, lo, m = PIECES[p]
        sec = 0 if way == RIGHT else CHUNK[c]
        return remote(
            xown.at[pl.ds(start_row[c] + lo, m), :], xc.at[c, pl.ds(sec + lo, m), :],
            ag_s.at[way, p], ag_r.at[way, p], way,
        )

    def fwd_piece(p, way):
        c, lo, m = PIECES[p]
        sec = 0 if way == RIGHT else CHUNK[c]
        cols = pl.ds(0 if way == RIGHT else half, half)
        return remote(
            xc.at[c, pl.ds(sec + lo, m), cols], xc.at[c, pl.ds(2 * CHUNK[c] + lo, m), cols],
            fw_s.at[way, p], fw_r.at[way, p], way,
        )

    def send_own(*ps):
        for p in ps:
            for way in (LEFT, RIGHT):
                own_piece(p, way).start()

    def forward(*ps):
        for p in ps:
            for way in (LEFT, RIGHT):
                own_piece(p, way).wait_recv()
                fwd_piece(p, way).start()

    def gathered(*ps):
        for p in ps:
            for way in (LEFT, RIGHT):
                fwd_piece(p, way).wait_recv()

    def hcol(j):
        return pl.ds(pl.multiple_of(j * TN, TN), TN)

    def acol(way, kind, j):
        first = (way == LEFT) == (kind != DIRECT)
        return pl.ds(pl.multiple_of((0 if first else half) + j * TN, TN), TN)

    def rs_copy(way, kind, c, j):
        r = pl.ds(start_row[c], CHUNK[c])
        if kind == DIAG:
            src, dst = ds.at[way, r, hcol(j)], dg.at[way, r, hcol(j)]
        else:
            cols = acol(way, kind, j)
            src, dst = st.at[way, r, cols], rc.at[way, r, cols]
        return remote(src, dst, rs_s.at[way, kind, c, j], rs_r.at[way, kind, c, j], way)

    def add_diag(c, j):
        m, r = CHUNK[c], pl.ds(start_row[c], CHUNK[c])
        for way in (LEFT, RIGHT):
            rs_copy(way, DIAG, c, j).wait_recv()
            total = lsum[way, pl.ds(0, m), hcol(j)] + dg[way, r, hcol(j)].astype(F32)
            st[way, r, acol(way, SUM, j)] = total.astype(BF)

    def send_sum(c, j):
        for way in (LEFT, RIGHT):
            rs_copy(way, SUM, c, j).start()

    def gate_up(lhs, m, h0, base, nxt, act):
        def body(i, carry):
            slot = lax.rem(base + i, SLOTS)
            for c in gu_copies(i, slot):
                c.wait()
            next_fetch("gu", n_gu, nxt, i, slot)
            act(i)
            acc = jnp.dot(lhs[pl.ds(0, m), :], ring[slot], preferred_element_type=F32)
            gate, up = acc[:, :TF], acc[:, TF:]
            h[pl.ds(h0, m), pl.ds(pl.multiple_of(i * TF, TF), TF)] = (jax.nn.silu(gate) * up).astype(BF)
            return carry

        lax.fori_loop(0, n_gu, body, 0)

    def down(c, h0, base, nxt, own, before, after):
        m = CHUNK[c]
        r = pl.ds(start_row[c], m)
        total = 3 * m + (rows if own else 0)

        def tile(j, which):
            t = 2 * j + which
            slot = lax.rem(base + t, SLOTS)
            for cp in dn_copies(t, slot):
                cp.wait()
            next_fetch("dn", n_dn, nxt, t, slot)
            return slot

        def product(slot, j, which):
            acc = jnp.dot(h[pl.ds(h0, total), :], ring[slot, pl.ds(0, ff), :], preferred_element_type=F32)
            diag_way = LEFT if which == 0 else RIGHT
            sec = (acc[0:m], acc[m:2 * m])
            ds[diag_way, r, hcol(j)] = acc[2 * m:3 * m].astype(BF)
            lsum[diag_way, pl.ds(0, m), hcol(j)] = sec[diag_way]
            st[1 - diag_way, r, acol(1 - diag_way, DIRECT, j)] = sec[1 - diag_way].astype(BF)
            if own:
                yown[:, pl.ds(pl.multiple_of(which * half + j * TN, TN), TN)] = acc[3 * m:]

        def send(j, which):
            diag_way = LEFT if which == 0 else RIGHT
            rs_copy(diag_way, DIAG, c, j).start()
            rs_copy(1 - diag_way, DIRECT, c, j).start()

        def body(j, carry):
            slot = tile(j, 0)

            @pl.when(j > 0)
            def _():
                send(j - 1, 1)

            before(j)
            product(slot, j, 0)
            slot = tile(j, 1)
            send(j, 0)
            after(j)
            product(slot, j, 1)
            return carry

        lax.fori_loop(0, pairs, body, 0)
        send(pairs - 1, 1)

    load = pltpu.make_async_copy(x, xown, xsem)
    load.start()
    for s in range(SLOTS - 1):
        fetch("gu", s, s)
    barrier = pltpu.get_barrier_semaphore()
    for way in (LEFT, RIGHT):
        pl.semaphore_signal(barrier, inc=1, device_id={"tp": peer[way]}, device_id_type=MESH)
    load.wait()
    pl.semaphore_wait(barrier, 2)
    send_own(0, 1)

    def act0(i):
        @pl.when(i == 9)
        def _():
            forward(0)

        @pl.when(i == 14)
        def _():
            forward(1)
            send_own(2, 3)

    gate_up(xown, rows, top, 0, "gu", act0)
    base = n_gu
    gathered(0, 1)

    def act1(i):
        @pl.when(i == 6)
        def _():
            forward(2)

        @pl.when(i == 11)
        def _():
            forward(3)
            send_own(4, 5)

    def sums(c, first):
        def act(i):
            k = i - first

            @pl.when((k >= 0) & (k < 2 * pairs))
            def _():
                @pl.when(lax.rem(k, 2) == 0)
                def _():
                    add_diag(c, k // 2)

                @pl.when(lax.rem(k, 2) == 1)
                def _():
                    send_sum(c, k // 2)

        return act

    sums0, sums1 = sums(0, 6), sums(1, 2)

    def act2(i):
        @pl.when(i == 1)
        def _():
            forward(4, 5)

        sums0(i)

    none = lambda j: None
    gate_up(xc.at[0], 3 * CHUNK[0], top - 3 * CHUNK[0], base, "dn", act1)
    base += n_gu
    down(0, top - 3 * CHUNK[0], base, "gu", False, none, none)
    base += n_dn
    gathered(2, 3)
    gate_up(xc.at[1], 3 * CHUNK[1], top - 3 * CHUNK[1], base, "dn", act2)
    base += n_gu
    down(1, top - 3 * CHUNK[1], base, "gu", False, none, none)
    base += n_dn
    gathered(4, 5)
    gate_up(xc.at[2], 3 * CHUNK[2], top - 3 * CHUNK[2], base, "dn", sums1)
    base += n_gu

    lag = 2

    def tail_add(j):
        @pl.when(j >= lag)
        def _():
            add_diag(2, j - lag)

    def tail_send(j):
        @pl.when(j >= lag)
        def _():
            send_sum(2, j - lag)

    down(2, top - 3 * CHUNK[2], base, None, True, tail_add, tail_send)

    def finish(j):
        for which in (0, 1):
            cols = pl.ds(pl.multiple_of(which * half + j * TN, TN), TN)
            for way in (LEFT, RIGHT):
                kind = SUM if (way == LEFT) == (which == 0) else DIRECT
                for c in range(len(CHUNK)):
                    rs_copy(way, kind, c, j).wait_recv()
            y[:, cols] = (yown[:, cols] + rc[LEFT, :, cols].astype(F32) + rc[RIGHT, :, cols].astype(F32)).astype(BF)

    def last_sums(j, carry):
        add_diag(2, j)
        finish(j - (pairs - lag))
        send_sum(2, j)
        return carry

    lax.fori_loop(pairs - lag, pairs, last_sums, 0)

    def finish_all(j, carry):
        finish(j)
        return carry

    lax.fori_loop(lag, pairs, finish_all, 0)

    for p in range(len(PIECES)):
        for way in (LEFT, RIGHT):
            own_piece(p, way).wait_send()
            fwd_piece(p, way).wait_send()
    for c in range(len(CHUNK)):
        def drain(j, carry, c=c):
            for way in (LEFT, RIGHT):
                for kind in (DIAG, DIRECT, SUM):
                    rs_copy(way, kind, c, j).wait_send()
            return carry

        lax.fori_loop(0, pairs, drain, 0)


def solution(mesh):
    def step(x, w_gate, w_up, w_down):
        rows, d = x.shape
        ff = w_gate.shape[1]
        half, pairs = d // 2, d // 2 // TN
        top = 3 * max(CHUNK)
        any_spec = pl.BlockSpec(memory_space=pl.ANY)
        dma = pltpu.SemaphoreType.DMA
        return pl.pallas_call(
            _kernel,
            out_shape=jax.ShapeDtypeStruct((rows, d), BF),
            in_specs=[any_spec] * 4,
            out_specs=pl.BlockSpec(memory_space=pltpu.VMEM),
            scratch_shapes=[
                pltpu.VMEM((rows, d), BF),
                pltpu.VMEM((len(CHUNK), top, d), BF),
                pltpu.VMEM((top + rows, ff), BF),
                pltpu.VMEM((SLOTS, d, max(2 * TF, TN)), BF),
                pltpu.VMEM((2, rows, half), BF),
                pltpu.VMEM((2, rows, half), BF),
                pltpu.VMEM((2, rows, d), BF),
                pltpu.VMEM((2, rows, d), BF),
                pltpu.VMEM((2, max(CHUNK), half), F32),
                pltpu.VMEM((rows, d), F32),
                dma(()),
                dma((SLOTS, 2)),
                dma((2, len(PIECES))),
                dma((2, len(PIECES))),
                dma((2, len(PIECES))),
                dma((2, len(PIECES))),
                dma((2, 3, len(CHUNK), pairs)),
                dma((2, 3, len(CHUNK), pairs)),
            ],
            compiler_params=pltpu.CompilerParams(
                collective_id=0, has_side_effects=True, vmem_limit_bytes=67_043_328
            ),
            cost_estimate=pl.CostEstimate(
                flops=6 * 4 * rows * d * ff, bytes_accessed=4 * 6 * d * ff, transcendentals=4 * rows * ff
            ),
        )(x, w_gate, w_up, w_down)

    return jax.shard_map(
        step,
        mesh=mesh,
        in_specs=(P(("dp", "tp"), None), P(None, "tp"), P(None, "tp"), P("tp", None)),
        out_specs=P(("dp", "tp"), None),
        check_vma=False,
    )
```

time: 340 us -> 176 us (0.52)
  waiting for transfers between devices: 175 us -> 0 us
  Pallas kernels: 0 us -> 173 us
  matrix products: 151 us -> 0 us
  between operations: 13.4 us -> 0.01 us
    pallas_call x0 -> x1, Pallas kernels: none -> 173 us  [step(): pl.pallas_call(_kernel, out_shape=jax.ShapeDtypeStruct((rows, d), BF), in...]
    dot_general x3 -> x0, matrix products: 151 us -> none  [the longest x1 53 us: step(): gate = jnp.dot(rows, w_gate, preferred_element_type=jnp.float32)]
    all_gather x1 -> x0, waiting for transfers between devices: 90.4 us -> none  [step(): rows = lax.all_gather(x, 'tp', axis=0, tiled=True)]
    reduce_scatter x1 -> x0, waiting for transfers between devices: 83.9 us -> none  [step(): return lax.psum_scatter(term, 'tp', scatter_dimension=0, tiled=True)]
  transfers between devices with their start and end apart: 2 -> 0, of which waited for: 2 -> 0; matrix products, arithmetic and copies ran while one was open for 0% -> 0% of each run, Pallas kernels for 0% -> 0%
where the time goes in v1:
time: 176 us
  Pallas kernels  173 us (98%)
  local copies, waits for them, and re-layouts  3.18 us (2%)
    pallas_call x1, Pallas kernels, step(): pl.pallas_call(_kernel, out_shape=jax.ShapeDtypeStruct((rows, d), BF), in...  173 us

profile of v1, /device:TPU:112, one launch (start us, length us, event | category | flops | bytes accessed | tf_op | source)
XLA Modules:
  0.0 176.4 jit_solution(15952502340288082421)
XLA Ops:
  0.0 173.2 %shard_map.46 = bf16[224,5120]{1,0:T(8,128)(2,1)} custom-call(bf16[224,5120]{1,0:T(8,128)(2,1)} %x.1, bf16[5120,4352]{1,0:T(8,128)(2,1)} %wg.1, bf16[5120,4352]{1,0:T(8,128)(2,1)} %wu.1, bf16[4352,5120]{1,0:T(8,128)(2,1)} %wd.1), custom_call_target="tpu_custom_call" | custom-call | flops 119789322240 | bytes 534773760 | tf_op jit(solution)/shard_map/pallas_call | solution.py:330
  173.2 3.2 %copy.6 = bf16[224,5120]{1,0:T(8,128)(2,1)} copy(bf16[224,5120]{1,0:T(8,128)(2,1)} %shard_map.46) | data formatting | bytes 4587520

commit v2 on v1

v2 whole, which is shorter than its diff:
```python
import functools

import jax
import jax.numpy as jnp
from jax import lax
from jax.experimental import pallas as pl
from jax.experimental.pallas import tpu as pltpu
from jax.sharding import PartitionSpec as P

BF = jnp.bfloat16
F32 = jnp.float32
MESH = pl.DeviceIdType.MESH
SLOTS = 6
TF = 256
TN = 512
CHUNK = (64, 96, 64)
PIECES = ((0, 0, 32), (0, 32, 32), (1, 0, 48), (1, 48, 48), (2, 0, 32), (2, 32, 32))
LEFT, RIGHT = 0, 1
DIAG, DIRECT, SUM = 0, 1, 2


def _kernel(
    x, wg, wu, wd, y,
    xown, xc, h, ring, ds, dg, st, rc, lsum, yown,
    xsem, wsem, ag_s, ag_r, fw_s, fw_r, rs_s, rs_r,
):
    rows, d = x.shape
    ff = wg.shape[1]
    half = d // 2
    n_gu = ff // TF
    pairs = half // TN
    n_dn = 2 * pairs
    start_row = [sum(CHUNK[:c]) for c in range(len(CHUNK))]
    top = 3 * max(CHUNK)

    me = lax.axis_index("tp")
    n = lax.axis_size("tp")
    peer = (lax.rem(me + n - 1, n), lax.rem(me + 1, n))

    def remote(src, dst, ssem, rsem, way):
        return pltpu.make_async_remote_copy(
            src_ref=src, dst_ref=dst, send_sem=ssem, recv_sem=rsem,
            device_id={"tp": peer[way]}, device_id_type=MESH,
        )

    def gu_copies(i, slot):
        cols = pl.ds(pl.multiple_of(i * TF, TF), TF)
        return (
            pltpu.make_async_copy(wg.at[:, cols], ring.at[slot, :, pl.ds(0, TF)], wsem.at[slot, 0]),
            pltpu.make_async_copy(wu.at[:, cols], ring.at[slot, :, pl.ds(TF, TF)], wsem.at[slot, 1]),
        )

    def dn_cols(t):
        return lax.rem(t, 2) * half + (t // 2) * TN

    def dn_copies(t, slot):
        cols = pl.ds(pl.multiple_of(dn_cols(t), TN), TN)
        return (pltpu.make_async_copy(wd.at[:, cols], ring.at[slot, pl.ds(0, ff), :], wsem.at[slot, 0]),)

    far = 100 * SLOTS + n_gu - 1

    def slot_up(q):
        return lax.rem(q, SLOTS)

    def slot_down(q):
        return lax.rem(far - q, SLOTS)

    def fetch(kind, i, slot):
        for c in (gu_copies if kind != "dn" else dn_copies)(n_gu - 1 - i if kind == "ug" else i, slot):
            c.start()

    def arrive(kind, i, slot):
        for c in (gu_copies if kind != "dn" else dn_copies)(n_gu - 1 - i if kind == "ug" else i, slot):
            c.wait()

    def fetch_ahead(kind, count, nxt, i, base, slot_of):
        if isinstance(i, int):
            if i < count:
                fetch(kind, i, slot_of(base + i))
            elif nxt is not None:
                fetch(nxt, i - count, slot_of(base + i))
            return

        @pl.when(i < count)
        def _():
            fetch(kind, i, slot_of(base + i))

        if nxt is not None:
            @pl.when(i >= count)
            def _():
                fetch(nxt, i - count, slot_of(base + i))

    def own_piece(p, way):
        c, lo, m = PIECES[p]
        sec = 0 if way == RIGHT else CHUNK[c]
        return remote(
            x.at[pl.ds(start_row[c] + lo, m), :], xc.at[pl.ds(3 * start_row[c] + sec + lo, m), :],
            ag_s.at[way, p], ag_r.at[way, p], way,
        )

    def fwd_piece(p, way):
        c, lo, m = PIECES[p]
        sec = 0 if way == RIGHT else CHUNK[c]
        cols = pl.ds(0 if way == RIGHT else half, half)
        return remote(
            xc.at[pl.ds(3 * start_row[c] + sec + lo, m), cols],
            xc.at[pl.ds(3 * start_row[c] + 2 * CHUNK[c] + lo, m), cols],
            fw_s.at[way, p], fw_r.at[way, p], way,
        )

    def send_own(*ps):
        for p in ps:
            for way in (LEFT, RIGHT):
                own_piece(p, way).start()

    def forward(*ps):
        for p in ps:
            for way in (LEFT, RIGHT):
                own_piece(p, way).wait_recv()
                fwd_piece(p, way).start()

    def gathered(*ps):
        for p in ps:
            for way in (LEFT, RIGHT):
                fwd_piece(p, way).wait_recv()

    def hcol(j):
        return pl.ds(pl.multiple_of(j * TN, TN), TN)

    def acol(way, kind, j):
        first = (way == LEFT) == (kind != DIRECT)
        return pl.ds(pl.multiple_of((0 if first else half) + j * TN, TN), TN)

    def rs_copy(way, kind, c, j):
        r = pl.ds(start_row[c], CHUNK[c])
        if kind == DIAG:
            src, dst = ds.at[way, r, hcol(j)], dg.at[way, r, hcol(j)]
        else:
            cols = acol(way, kind, j)
            src, dst = st.at[way, r, cols], rc.at[way, r, cols]
        return remote(src, dst, rs_s.at[way, kind, c, j], rs_r.at[way, kind, c, j], way)

    def add_diag(c, j):
        m, r = CHUNK[c], pl.ds(start_row[c], CHUNK[c])
        for way in (LEFT, RIGHT):
            rs_copy(way, DIAG, c, j).wait_recv()
            total = lsum[way, pl.ds(0, m), hcol(j)] + dg[way, r, hcol(j)].astype(F32)
            st[way, r, acol(way, SUM, j)] = total.astype(BF)

    def send_sum(c, j):
        for way in (LEFT, RIGHT):
            rs_copy(way, SUM, c, j).start()

    def gate_up(lhs, r0, m, h0, kind, base, slot_of, nxt, act, after_pair=False):
        def body(i, carry):
            slot = slot_of(base + i)
            if kind == "ug":
                @pl.when(i >= SLOTS)
                def _():
                    arrive(kind, i, slot)

                @pl.when(i >= 1)
                def _():
                    fetch_ahead(kind, n_gu, nxt, i + SLOTS - 1, base, slot_of)
            else:
                arrive(kind, i, slot)
                if after_pair:
                    @pl.when(i == 0)
                    def _():
                        fetch(kind, SLOTS - 2, slot_of(base + SLOTS - 2))
                fetch_ahead(kind, n_gu, nxt, i + SLOTS - 1, base, slot_of)
            act(i)
            hidden(lhs, r0, m, h0, kind, i, slot)
            return carry

        lax.fori_loop(0, n_gu, body, 0)

    def hidden(lhs, r0, m, h0, kind, i, slot):
        acc = jnp.dot(lhs[pl.ds(r0, m), :], ring[slot], preferred_element_type=F32)
        gate, up = acc[:, :TF], acc[:, TF:]
        tile = n_gu - 1 - i if kind == "ug" else i
        cols = pl.ds(tile * TF if isinstance(tile, int) else pl.multiple_of(tile * TF, TF), TF)
        h[pl.ds(h0, m), cols] = (jax.nn.silu(gate) * up).astype(BF)

    def gate_up_pairs(lhs, r0, m, h0, base, nxt, act):
        def body(k, carry):
            i = 2 * k
            for w in (0, 1):
                arrive("gu", i + w, slot_down(base + i + w))

            @pl.when(k > 0)
            def _():
                fetch_ahead("gu", n_gu, nxt, i + SLOTS - 2, base, slot_down)

            fetch_ahead("gu", n_gu, nxt, i + SLOTS - 1, base, slot_down)
            act(k)
            for w in (0, 1):
                hidden(lhs, r0, m, h0, "gu", i + w, slot_down(base + i + w))
            return carry

        lax.fori_loop(0, n_gu // 2, body, 0)
        i = n_gu - 1
        arrive("gu", i, slot_down(base + i))
        for a in (SLOTS - 2, SLOTS - 1):
            fetch_ahead("gu", n_gu, nxt, i + a, base, slot_down)
        hidden(lhs, r0, m, h0, "gu", i, slot_down(base + i))

    def kind_of(way, which):
        return SUM if (way == LEFT) == (which == 0) else DIRECT

    def terms(c, acc, j, which):
        m = CHUNK[c]
        r = pl.ds(start_row[c], m)
        diag_way = LEFT if which == 0 else RIGHT
        sec = (acc[0:m], acc[m:2 * m])
        ds[diag_way, r, hcol(j)] = acc[2 * m:3 * m].astype(BF)
        lsum[diag_way, pl.ds(0, m), hcol(j)] = sec[diag_way]
        st[1 - diag_way, r, acol(1 - diag_way, DIRECT, j)] = sec[1 - diag_way].astype(BF)

    def own_rows(acc, j, which):
        cols = pl.ds(pl.multiple_of(which * half + j * TN, TN), TN)
        early = rows - CHUNK[-1]
        for c in range(len(CHUNK) - 1):
            for way in (LEFT, RIGHT):
                rs_copy(way, kind_of(way, which), c, j).wait_recv()
        y[pl.ds(0, early), cols] = (
            acc[:early]
            + rc[LEFT, pl.ds(0, early), cols].astype(F32)
            + rc[RIGHT, pl.ds(0, early), cols].astype(F32)
        ).astype(BF)
        yown[:, cols] = acc[early:]

    def product(slot, r0, m):
        return jnp.dot(h[pl.ds(r0, m), :], ring[slot, pl.ds(0, ff), :], preferred_element_type=F32)

    def send_terms(c, j, which):
        diag_way = LEFT if which == 0 else RIGHT
        rs_copy(diag_way, DIAG, c, j).start()
        rs_copy(1 - diag_way, DIRECT, c, j).start()

    def down(c, base, nxt, act):
        def body(j, carry):
            for w in (0, 1):
                t = 2 * j + w
                slot = slot_down(base + t)
                arrive("dn", t, slot)
                fetch_ahead("dn", n_dn, nxt, t + SLOTS - 1, base, slot_down)
                if w == 1:
                    send_terms(c, j, 0)
                else:
                    @pl.when(j > 0)
                    def _():
                        send_terms(c, j - 1, 1)
                    act(j)
                terms(c, product(slot, h0[c], 3 * CHUNK[c]), j, w)
            return carry

        lax.fori_loop(0, pairs, body, 0)
        send_terms(c, pairs - 1, 1)

    def down_pairs(c, base, nxt):
        def body(j, carry):
            t = 2 * j
            slots = [slot_down(base + t + w) for w in (0, 1)]
            for w in (0, 1):
                arrive("dn", t + w, slots[w])

            @pl.when(j > 0)
            def _():
                fetch_ahead("dn", n_dn, nxt, t + SLOTS - 2, base, slot_down)

            fetch_ahead("dn", n_dn, nxt, t + SLOTS - 1, base, slot_down)

            @pl.when(j > 0)
            def _():
                for w in (0, 1):
                    send_terms(c, j - 1, w)

            for w in (0, 1):
                terms(c, product(slots[w], h0[c], 3 * CHUNK[c]), j, w)
            return carry

        lax.fori_loop(0, pairs, body, 0)
        for w in (0, 1):
            send_terms(c, pairs - 1, w)

    def down_last(c, base):
        def tile(t):
            slot = slot_down(base + t)
            arrive("dn", t, slot)

            @pl.when(t + SLOTS - 1 < n_dn)
            def _():
                fetch("dn", t + SLOTS - 1, slot_down(base + t + SLOTS - 1))

            return slot

        m3 = 3 * CHUNK[c]

        def both(j, carry):
            for w in (0, 1):
                slot = tile(2 * j + w)
                if w == 1:
                    send_terms(c, j, 0)

                    @pl.when(j >= lag)
                    def _():
                        send_sum(c, j - lag)
                else:
                    @pl.when(j > 0)
                    def _():
                        send_terms(c, j - 1, 1)

                    @pl.when(j >= lag)
                    def _():
                        add_diag(c, j - lag)
                acc = product(slot, h0[c], m3 + rows)
                terms(c, acc[:m3], j, w)
                own_rows(acc[m3:], j, w)
            return carry

        def peers(j, carry):
            for w in (0, 1):
                slot = tile(2 * j + w)
                if w == 1:
                    send_terms(c, j, 0)
                    send_sum(c, j - lag)
                else:
                    send_terms(c, j - 1, 1)
                    add_diag(c, j - lag)
                terms(c, product(slot, h0[c], m3), j, w)
            return carry

        def mine(j, carry):
            for w in (0, 1):
                if w == 1:
                    @pl.when(j == split)
                    def _():
                        add_diag(c, split)
                else:
                    @pl.when(j == split)
                    def _():
                        send_terms(c, pairs - 1, 1)

                    @pl.when(j > split)
                    def _():
                        send_sum(c, split)
                own_rows(product(slot_down(base + 2 * j + w), top, rows), j, w)
            return carry

        split = pairs - lag
        lax.fori_loop(0, split, both, 0)
        lax.fori_loop(split, pairs, peers, 0)
        lax.fori_loop(split, pairs, mine, 0)

    h0 = [top - 3 * m for m in CHUNK]
    lag = 2

    barrier = pltpu.get_barrier_semaphore()
    for way in (LEFT, RIGHT):
        pl.semaphore_signal(barrier, inc=1, device_id={"tp": peer[way]}, device_id_type=MESH)
    load = pltpu.make_async_copy(x, xown, xsem)
    load.start()
    fetch("gu", 0, slot_up(0))
    pl.semaphore_wait(barrier, 2)
    send_own(0)
    load.wait()
    for i in range(1, SLOTS - 1):
        fetch("gu", i, slot_up(i))

    def at(step, i, *do):
        @pl.when(i == step)
        def _():
            for f, ps in do:
                f(*ps)

    def act0(i):
        at(3, i, (send_own, (1,)))
        at(7, i, (forward, (0,)))
        at(11, i, (forward, (1,)))
        at(13, i, (send_own, (2,)))

    gate_up(xown, 0, rows, top, "gu", 0, slot_up, None, act0)
    gathered(0, 1)

    def act1(i):
        at(3, i, (send_own, (3,)))
        at(8, i, (forward, (2,)))

    def act1d(j):
        at(0, j, (forward, (3,)))

    def sums(c, first):
        def act(k):
            @pl.when((k > first) & (k <= first + pairs))
            def _():
                send_sum(c, k - first - 1)

            @pl.when((k >= first) & (k < first + pairs))
            def _():
                add_diag(c, k - first)

        return act

    def drain_gather():
        for p in range(len(PIECES)):
            for way in (LEFT, RIGHT):
                own_piece(p, way).wait_send()
                fwd_piece(p, way).wait_send()

    def drain_terms(c):
        def body(j, carry):
            for way in (LEFT, RIGHT):
                for kind in (DIAG, DIRECT, SUM):
                    rs_copy(way, kind, c, j).wait_send()
            return carry

        lax.fori_loop(0, pairs, body, 0)

    sums0 = sums(0, 2)

    def act2(k):
        at(0, k, (send_own, (4, 5)))
        at(7, k, (forward, (4, 5)))
        sums0(k)

    def act3(i):
        k = i - 2

        @pl.when((k >= 0) & (k < 2 * pairs))
        def _():
            @pl.when(lax.rem(k, 2) == 0)
            def _():
                add_diag(1, k // 2)

            @pl.when(lax.rem(k, 2) == 1)
            def _():
                send_sum(1, k // 2)

        at(13, i, (drain_gather, ()))
        at(14, i, (drain_terms, (0,)))

    base = 0
    gate_up(xc, 0, 3 * CHUNK[0], h0[0], "ug", base, slot_down, "dn", act1)
    base += n_gu
    down(0, base, "gu", act1d)
    base += n_dn
    gathered(2, 3)
    gate_up_pairs(xc, 3 * start_row[1], 3 * CHUNK[1], h0[1], base, "dn", act2)
    base += n_gu
    down_pairs(1, base, "gu")
    base += n_dn
    gathered(4, 5)
    gate_up(xc, 3 * start_row[2], 3 * CHUNK[2], h0[2], "gu", base, slot_down, "dn", act3, after_pair=True)
    base += n_gu
    down_last(2, base)

    last = pl.ds(start_row[2], CHUNK[2])

    def finish(j):
        for which in (0, 1):
            cols = pl.ds(pl.multiple_of(which * half + j * TN, TN), TN)
            for way in (LEFT, RIGHT):
                rs_copy(way, kind_of(way, which), 2, j).wait_recv()
            y[last, cols] = (
                yown[:, cols] + rc[LEFT, last, cols].astype(F32) + rc[RIGHT, last, cols].astype(F32)
            ).astype(BF)

    add_diag(2, pairs - 1)
    for j in range(lag):
        finish(j)
    send_sum(2, pairs - 1)
    drain_terms(1)

    def finish_all(j, carry):
        finish(j)
        return carry

    lax.fori_loop(lag, pairs, finish_all, 0)
    drain_terms(2)


def solution(mesh):
    def step(x, w_gate, w_up, w_down):
        rows, d = x.shape
        ff = w_gate.shape[1]
        half, pairs = d // 2, d // 2 // TN
        top = 3 * max(CHUNK)
        any_spec = pl.BlockSpec(memory_space=pl.ANY)
        dma = pltpu.SemaphoreType.DMA
        return pl.pallas_call(
            _kernel,
            out_shape=pltpu.VMEM((rows, d), BF),
            in_specs=[any_spec] * 4,
            out_specs=pl.BlockSpec(memory_space=pltpu.VMEM),
            scratch_shapes=[
                pltpu.VMEM((rows, d), BF),
                pltpu.VMEM((3 * rows, d), BF),
                pltpu.VMEM((top + rows, ff), BF),
                pltpu.VMEM((SLOTS, d, max(2 * TF, TN)), BF),
                pltpu.VMEM((2, rows, half), BF),
                pltpu.VMEM((2, rows, half), BF),
                pltpu.VMEM((2, rows, d), BF),
                pltpu.VMEM((2, rows, d), BF),
                pltpu.VMEM((2, max(CHUNK), half), F32),
                pltpu.VMEM((CHUNK[-1], d), F32),
                dma(()),
                dma((SLOTS, 2)),
                dma((2, len(PIECES))),
                dma((2, len(PIECES))),
                dma((2, len(PIECES))),
                dma((2, len(PIECES))),
                dma((2, 3, len(CHUNK), pairs)),
                dma((2, 3, len(CHUNK), pairs)),
            ],
            compiler_params=pltpu.CompilerParams(
                collective_id=0, has_side_effects=True, vmem_limit_bytes=64_600_000
            ),
            cost_estimate=pl.CostEstimate(
                flops=6 * 4 * rows * d * ff, bytes_accessed=4 * 6 * d * ff, transcendentals=4 * rows * ff
            ),
        )(x, w_gate, w_up, w_down)

    return jax.shard_map(
        step,
        mesh=mesh,
        in_specs=(P(("dp", "tp"), None), P(None, "tp"), P(None, "tp"), P("tp", None)),
        out_specs=P(("dp", "tp"), None),
        check_vma=False,
    )
```

time: 176 us -> 166 us (0.943)
  Pallas kernels: 173 us -> 164 us
  local copies, waits for them, and re-layouts: 3.18 us -> 1.39 us
    pallas_call x1, Pallas kernels: 173 us -> 164 us  [step(): pl.pallas_call(_kernel, out_shape=pltpu.VMEM((rows, d), BF), in_specs=[an...]
    unnamed x1, local copies, waits for them, and re-layouts: 3.18 us -> 1.39 us
where the time goes in v2:
time: 166 us
  Pallas kernels  164 us (99%)
    pallas_call x1, Pallas kernels, step(): pl.pallas_call(_kernel, out_shape=pltpu.VMEM((rows, d), BF), in_specs=[an...  164 us

profile of v2, /device:TPU:112, one launch (start us, length us, event | category | flops | bytes accessed | tf_op | source)
XLA Modules:
  0.0 165.8 jit_solution(1168966855037575035)
XLA Ops:
  0.0 164.4 %shard_map.46 = bf16[224,5120]{1,0:T(8,128)(2,1)S(1)} custom-call(bf16[224,5120]{1,0:T(8,128)(2,1)} %x.1, bf16[5120,4352]{1,0:T(8,128)(2,1)} %wg.1, bf16[5120,4352]{1,0:T(8,128)(2,1)} %wu.1, bf16[4352,5120]{1,0:T(8,128)(2,1)} %wd.1), custom_call_target="tpu_custom_call" | custom-call | flops 119789322240 | bytes 534773760 | tf_op jit(solution)/shard_map/pallas_call | solution.py:491
  164.4 1.4 copy.6
